TPU v7x, 32 devices: a whole 2x2x4 slice. The times are simulated.
32 devices in a mesh: row: 4 (over z), col: 8 (over y, x, core).
Axes of the slice: x: 2, y: 2, z: 4, core: 2. Of those that a mesh axis runs over, the one named last changes fastest.
Arguments:
- momentum: float32 [8192, 26624], P('row', 'col'), may hold values from -6 to 6
- gradient: bfloat16 [8192, 26624], P('row', 'col'), may hold values from -150 to 150
- q_basis: bfloat16 [26624, 512], P('col', 'row'), may hold values from -0.0390625 to 0.0390625
Outputs:
- momentum_next: float32 [8192, 26624], P('row', 'col')
- p_basis: float32 [8192, 512], P(('row', 'col'))
- q_next: float32 [26624, 512], P('col', 'row')
All inputs are finite; a program needn't handle non-finite values.
Results may differ from a plain program's by a relative error of at most 0.0065.
Values may be sent and summed in bfloat16 or wider, within the bound.
No kernel may reach another device: no remote copies, remote signals or barrier semaphores. Data moves between devices by JAX's collectives and lax.ppermute only.
A program may use at most 128 MiB of HBM per device.

v0:
```python
import jax
import jax.numpy as jnp
from jax import lax
from jax.sharding import PartitionSpec as P


def body(momentum, gradient, q_basis):
    buffer = momentum + gradient.astype(jnp.float32)
    buffer_low = buffer.astype(jnp.bfloat16)
    power_part = jnp.dot(
        buffer_low,
        lax.all_gather(q_basis, "row", axis=1, tiled=True),
        preferred_element_type=jnp.float32,
    )
    row_share = buffer.shape[0] // lax.axis_size("col")
    col_index = lax.axis_index("col")
    power = lax.psum(power_part, "col")
    local_gram = jnp.dot(power.T, power, precision=lax.Precision.HIGHEST)
    gram = lax.psum(local_gram, "row")
    lower = jnp.linalg.cholesky(gram)
    p_full = jax.scipy.linalg.solve_triangular(lower, power.T, lower=True).T
    p_low = p_full.astype(jnp.bfloat16)
    p_out = lax.dynamic_slice_in_dim(p_full, col_index * row_share, row_share, 0)
    right_part = jnp.einsum("ic,ir->cr", buffer_low, p_low, preferred_element_type=jnp.float32)
    right_cols = lax.psum_scatter(right_part, "row", scatter_dimension=1, tiled=True)
    sums = lax.psum(jnp.sum(right_cols * right_cols, axis=0), "col")
    q_next = right_cols / jnp.sqrt(sums + 1e-06)
    right_low = lax.all_gather(right_cols.astype(jnp.bfloat16), "row", axis=1, tiled=True)
    update = jnp.einsum("ir,cr->ic", p_low, right_low, preferred_element_type=jnp.float32)
    return (buffer - 0.1 * update, p_out, q_next)


def solution(mesh):
    return jax.shard_map(
        body,
        mesh=mesh,
        in_specs=(P("row", "col"), P("row", "col"), P("col", "row")),
        out_specs=(P("row", "col"), P(("row", "col"), None), P("col", "row")),
        check_vma=False,
    )
```

profile of v0, /device:TPU:0, one launch (start us, length us, event | category | flops | bytes accessed | tf_op | source)
XLA Modules:
  0.0 653.8 jit_solution(9504467316959625717)
XLA Ops:
  7.9 72.0 %all-gather.3.cloned.1.call-done = bf16[3328,512]{1,0:T(8,128)(2,1)} async-done(((bf16[3328,128]{1,0:T(8,128)(2,1)}), bf16[3328,512]{1,0:T(8,128)(2,1)}) %all-gather.3.cloned.1.call-update) | async-done | bytes 3407888 | tf_op jit(solution)/shard_map/all_gather | solution.py:12
  80.0 19.4 %fusion.39 = f32[2048,512]{1,0:T(8,128)} fusion(bf16[3328,512]{1,0:T(8,128)(2,1)} %all-gather.3.cloned.1.call-done, f32[2048,3328]{1,0:T(8,128)} %param.3, bf16[2048,3328]{1,0:T(8,128)(2,1)} %param.4), kind=kOutput, calls=%fused_computation.77 | convolution fusion | flops 6999769088 | bytes 48496640 | tf_op jit(solution)/shard_map/dot_general | solution.py:10
  99.4 79.1 %all-reduce.4.cloned.1.call-done = f32[2048,512]{1,0:T(8,128)} async-done(((f32[2048,512]{1,0:T(8,128)}), f32[2048,512]{1,0:T(8,128)}) %all-reduce.4.cloned.1.call-update) | async-done | bytes 4194320 | tf_op jit(solution)/shard_map/psum | solution.py:17
  178.5 11.4 %fusion.42 = f32[512,512]{0,1:T(8,128)} fusion(f32[2048,512]{1,0:T(8,128)} %all-reduce.4.cloned.1.call-done), kind=kOutput, calls=%fused_computation.79 | convolution fusion | flops 6442450944 | bytes 5242880 | tf_op jit(solution)/shard_map/dot_general | solution.py:18
  190.2 51.9 %all-reduce.6.cloned.1.call-done = f32[512,512]{0,1:T(8,128)} async-done(((f32[512,512]{0,1:T(8,128)}), f32[512,512]{0,1:T(8,128)}) %all-reduce.6.cloned.1.call-update) | async-done | bytes 1048592 | tf_op jit(solution)/shard_map/psum | solution.py:19
  245.1 11.7 %cholesky.104 = f32[128,128]{1,0:T(8,128)S(1)} custom-call(f32[128,128]{1,0:T(8,128)S(1)} %cholesky.266), custom_call_target="Cholesky" | custom-call | tf_op jit(solution)/shard_map/jit(cholesky)/cholesky | solution.py:20
  256.8 9.8 %custom-call.31 = f32[1,128,128]{1,2,0:T(8,128)S(1)} custom-call(f32[1,128,128]{2,1,0:T(8,128)S(1)} %get-tuple-element.35), custom_call_target="InvertDiagBlocksLowerTriangular" | custom-call | tf_op jit(solution)/shard_map/jit(cholesky)/cholesky | solution.py:20
  267.4 11.7 %cholesky.217 = f32[128,128]{1,0:T(8,128)S(1)} custom-call(f32[128,128]{1,0:T(8,128)S(1)} %cholesky.270), custom_call_target="Cholesky" | custom-call | tf_op jit(solution)/shard_map/jit(cholesky)/cholesky | solution.py:20
  279.2 10.2 %custom-call.32 = f32[1,128,128]{1,2,0:T(8,128)S(1)} custom-call(f32[1,128,128]{2,1,0:T(8,128)S(1)} %get-tuple-element.32), custom_call_target="InvertDiagBlocksLowerTriangular" | custom-call | tf_op jit(solution)/shard_map/jit(cholesky)/cholesky | solution.py:20
  290.1 11.7 %cholesky.238 = f32[128,128]{1,0:T(8,128)S(1)} custom-call(f32[128,128]{1,0:T(8,128)S(1)} %cholesky.275), custom_call_target="Cholesky" | custom-call | tf_op jit(solution)/shard_map/jit(cholesky)/cholesky | solution.py:20
  302.5 9.8 %custom-call.33 = f32[1,128,128]{1,2,0:T(8,128)S(1)} custom-call(f32[1,128,128]{2,1,0:T(8,128)S(1)} %get-tuple-element.29), custom_call_target="InvertDiagBlocksLowerTriangular" | custom-call | tf_op jit(solution)/shard_map/jit(cholesky)/cholesky | solution.py:20
  312.9 11.7 %cholesky.255 = f32[128,128]{1,0:T(8,128)S(1)} custom-call(f32[128,128]{1,0:T(8,128)S(1)} %convolution_subtract_fusion.4), custom_call_target="Cholesky" | custom-call | tf_op jit(solution)/shard_map/jit(cholesky)/cholesky | solution.py:20
  328.9 10.4 %while.1 = (s32[]{:T(128)}, f32[512,512]{1,0:T(8,128)S(1)}, s32[4,2]{0,1:T(2,128)S(1)}, f32[4,128,128]{2,1,0:T(8,128)}, s32[]{:T(128)}) while((s32[]{:T(128)}, f32[512,512]{1,0:T(8,128)S(1)}, s32[4,2]{0,1:T(2,128)S(1)}, f32[4,128,128]{2,1,0:T(8,128)}, s32[]{:T(128)}) %tuple.33), condition=%wide.while_cond, body=%wide.while_body.sunk | while | flops 2 | bytes 132205 | solution.py:21
  339.2 40.2 %custom-call.34 = f32[4,128,128]{1,2,0:T(8,128)S(1)} custom-call(f32[4,128,128]{2,1,0:T(8,128)} %get-tuple-element.10), custom_call_target="InvertDiagBlocksLowerTriangular" | custom-call | tf_op jit(solution)/shard_map/jit(_solve_triangular)/triangular_solve | solution.py:21
  379.4 2.4 fusion.13
  381.9 3.0 convolution_subtract_fusion.1
  386.0 3.5 convolution_subtract_fusion
  390.6 6.5 fusion.7
  399.2 19.7 %fusion.17 = f32[3328,512]{1,0:T(8,128)} fusion(f32[2048,3328]{1,0:T(8,128)} %param.3, bf16[2048,3328]{1,0:T(8,128)(2,1)} %param.4, f32[128,2048]{1,0:T(8,128)} %fusion.27, f32[128,2048]{1,0:T(8,128)S(1)} %fusion.28, f32[128,2048]{1,0:T(8,128)S(1)} %fusion.30, f32[128,2048]{1,0:T(8,128)S(1)} %fusion.13), kind=kOutput, calls=%fused_computation.30 | convolution fusion | flops 7008157696 | bytes 51904512 | tf_op jit(solution)/shard_map/ic,ir->cr/dot_general | solution.py:24
  419.0 118.7 %reduce-scatter.2.cloned.1.call-done = f32[3328,128]{1,0:T(8,128)} async-done(((f32[3328,512]{1,0:T(8,128)}), f32[3328,128]{1,0:T(8,128)}) %reduce-scatter.2.cloned.1.call-update) | async-done | bytes 1703952 | tf_op jit(solution)/shard_map/reduce_scatter | solution.py:25
  539.5 13.6 %psum.23 = f32[128]{0:T(128)S(1)} all-reduce(f32[128]{0:T(128)S(1)} %multiply_reduce_fusion), channel_id=1, replica_groups=mesh['row'=4,'col'=8] {'col'}, use_global_device_ids=true, to_apply=%region_12.13 | all-reduce | flops 128 | bytes 1024 | tf_op jit(solution)/shard_map/psum | solution.py:26
  553.1 3.7 broadcast_divide_fusion
  561.2 62.1 %all-gather.5.cloned.1.call-done = bf16[3328,512]{1,0:T(8,128)(2,1)} async-done(((bf16[3328,128]{1,0:T(8,128)(2,1)}), bf16[3328,512]{1,0:T(8,128)(2,1)}) %all-gather.5.cloned.1.call-update) | async-done | bytes 3407888 | tf_op jit(solution)/shard_map/all_gather | solution.py:28
  623.3 23.8 %multiply_subtract_fusion = f32[2048,3328]{1,0:T(8,128)} fusion(f32[2048,3328]{1,0:T(8,128)} %param.3, bf16[2048,3328]{1,0:T(8,128)(2,1)} %param.4, bf16[3328,512]{1,0:T(8,128)(2,1)} %all-gather.5.cloned.1.call-done, f32[128,2048]{1,0:T(8,128)} %fusion.27, f32[128,2048]{1,0:T(8,128)S(1)} %fusion.28, f32[128,2048]{1,0:T(8,128)S(1)} %fusion.30, ...), kind=kOutput, calls=%fused_computation.2 | convolution fusion | flops 7014973440 | bytes 75759616 | tf_op jit(solution)/shard_map/ir,cr->ic/dot_general | solution.py:29
  (57 shorter events, 29.5 us)
Async XLA Ops:
  7.2 72.8 %all-gather.3.cloned.1.call-start = ((), (), s32[]{:S(2)}) async-start(), calls=%async_computation.1 | async-start | bytes 4259840 | tf_op jit(solution)/shard_map/all_gather | solution.py:12
  7.9 170.6 %all-reduce.4.cloned.1.call-start = ((), (), s32[]{:S(2)}) async-start(), calls=%async_computation.2 | async-start | bytes 8388608 | tf_op jit(solution)/shard_map/psum | solution.py:17
  99.4 142.7 %all-reduce.6.cloned.1.call-start = ((), (), s32[]{:S(2)}) async-start(), calls=%async_computation.3 | async-start | bytes 2097152 | tf_op jit(solution)/shard_map/psum | solution.py:19
  189.9 347.7 %reduce-scatter.2.cloned.1.call-start = ((), (), s32[]{:S(2)}) async-start(), calls=%async_computation.4 | async-start | bytes 8519680 | tf_op jit(solution)/shard_map/reduce_scatter | solution.py:25
  339.2 46.8 %copy-start.1 = (f32[512,512]{1,0:T(8,128)}, f32[512,512]{1,0:T(8,128)S(1)}, u32[]{:S(2)}) copy-start(f32[512,512]{1,0:T(8,128)S(1)} %get-tuple-element.101) | copy-start | bytes 3145732
  379.4 6.6 %copy-start = (f32[2048,512]{1,0:T(8,128)S(1)}, f32[2048,512]{1,0:T(8,128)}, u32[]{:S(2)}) copy-start(f32[2048,512]{1,0:T(8,128)} %all-reduce.4.cloned.1.call-done) | copy-start | bytes 12582916
  418.9 204.4 %all-gather.5.cloned.1.call-start = ((), (), s32[]{:S(2)}) async-start(), calls=%async_computation.5 | async-start | bytes 4259840 | tf_op jit(solution)/shard_map/all_gather | solution.py:28
Sparse Core Ops, SparseCore 0:
  9.5 70.3 all-gather.2
  99.5 78.9 all-reduce.3
  190.1 51.9 all-reduce.5
  419.0 118.5 reduce-scatter.1
  556.9 66.3 all-gather.4
where the time goes:
time: 660 us; the launch traced here: 654 us
  waiting for transfers between devices  384 us (58%)
  other arithmetic  128 us (19%)
  matrix products  95.8 us (15%)
  between operations  16.8 us (3%)
  local copies, waits for them, and re-layouts  14.9 us (2%)
  blocking collectives  13.6 us (2%)
    reduce_scatter x1, waiting for transfers between devices, body(): lax.psum_scatter(right_part, 'row', scatter_dimension=1, tiled=True)  119 us
    psum x1, waiting for transfers between devices, body(): power = lax.psum(power_part, 'col')  79.1 us
    another operation x14, other arithmetic, body(): lower = jnp.linalg.cholesky(gram)  78.8 us
    all_gather x1, waiting for transfers between devices, body(): lax.all_gather(q_basis, 'row', axis=1, tiled=True)  72 us
    all_gather x1, waiting for transfers between devices, body(): lax.all_gather(right_cols.astype(jnp.bfloat16), 'row', axis=1, tiled=True)  62.1 us
    psum x1, waiting for transfers between devices, body(): gram = lax.psum(local_gram, 'row')  51.9 us
    another operation x4, other arithmetic, body(): p_full = jax.scipy.linalg.solve_triangular(lower, power.T, lower=True).T  42 us
    dot_general x1, matrix products, body(): jnp.einsum('ir,cr->ic', p_low, right_low, preferred_element_type=jnp.floa...  23.8 us
  transfers between devices with their start and end apart: 5, of which 5 were waited for; matrix products, arithmetic and copies ran while one was open for 1% of the time, Pallas kernels for 0%

commit v1 on v0

--- a/solution.py
+++ b/solution.py
@@ -14,7 +14,7 @@
     )
     row_share = buffer.shape[0] // lax.axis_size("col")
     col_index = lax.axis_index("col")
-    power = lax.psum(power_part, "col")
+    power = jnp.sum(lax.all_gather(power_part, "col"), axis=0)
     local_gram = jnp.dot(power.T, power, precision=lax.Precision.HIGHEST)
     gram = lax.psum(local_gram, "row")
     lower = jnp.linalg.cholesky(gram)

time: 660 us -> 756 us (1.15)
  waiting for transfers between devices: 384 us -> 464 us
  other arithmetic: 128 us -> 143 us
    all_gather x0 -> x1, waiting for transfers between devices: none -> 159 us  [body(): power = jnp.sum(lax.all_gather(power_part, 'col'), axis=0)]
    psum x1 -> x0, waiting for transfers between devices: 79.1 us -> none  [body(): power = lax.psum(power_part, 'col')]
    reduce_sum x0 -> x1, other arithmetic: none -> 15.1 us  [body(): power = jnp.sum(lax.all_gather(power_part, 'col'), axis=0)]
where the time goes in v1:
time: 756 us; the launch traced here: 749 us
  waiting for transfers between devices  464 us (61%)
  other arithmetic  143 us (19%)
  matrix products  96 us (13%)
  between operations  16.8 us (2%)
  local copies, waits for them, and re-layouts  15.5 us (2%)
  blocking collectives  13.5 us (2%)
    all_gather x1, waiting for transfers between devices, body(): power = jnp.sum(lax.all_gather(power_part, 'col'), axis=0)  159 us
    reduce_scatter x1, waiting for transfers between devices, body(): lax.psum_scatter(right_part, 'row', scatter_dimension=1, tiled=True)  119 us
    another operation x14, other arithmetic, body(): lower = jnp.linalg.cholesky(gram)  78.8 us
    all_gather x1, waiting for transfers between devices, body(): lax.all_gather(q_basis, 'row', axis=1, tiled=True)  72 us
    all_gather x1, waiting for transfers between devices, body(): lax.all_gather(right_cols.astype(jnp.bfloat16), 'row', axis=1, tiled=True)  62.1 us
    psum x1, waiting for transfers between devices, body(): gram = lax.psum(local_gram, 'row')  51.8 us
    another operation x4, other arithmetic, body(): p_full = jax.scipy.linalg.solve_triangular(lower, power.T, lower=True).T  42 us
    dot_general x1, matrix products, body(): jnp.einsum('ir,cr->ic', p_low, right_low, preferred_element_type=jnp.floa...  23.8 us
  transfers between devices with their start and end apart: 5, of which 5 were waited for; matrix products, arithmetic and copies ran while one was open for 1% of the time, Pallas kernels for 0%

profile of v1, /device:TPU:0, one launch (start us, length us, event | category | flops | bytes accessed | tf_op | source)
XLA Modules:
  0.0 749.4 jit_solution(10172843686284890210)
XLA Ops:
  7.9 72.0 %all-gather.5.cloned.1.call-done = bf16[3328,512]{1,0:T(8,128)(2,1)} async-done(((bf16[3328,128]{1,0:T(8,128)(2,1)}), bf16[3328,512]{1,0:T(8,128)(2,1)}) %all-gather.5.cloned.1.call-update) | async-done | bytes 3407888 | tf_op jit(solution)/shard_map/all_gather | solution.py:12
  80.0 19.4 %fusion.39 = f32[2048,512]{1,0:T(8,128)} fusion(bf16[3328,512]{1,0:T(8,128)(2,1)} %all-gather.5.cloned.1.call-done, f32[2048,3328]{1,0:T(8,128)} %param.3, bf16[2048,3328]{1,0:T(8,128)(2,1)} %param.4), kind=kOutput, calls=%fused_computation.77 | convolution fusion | flops 6999769088 | bytes 48496640 | tf_op jit(solution)/shard_map/dot_general | solution.py:10
  99.4 159.0 %all-gather.9.cloned.1.call-done = f32[16384,512]{1,0:T(8,128)} async-done(((f32[2048,512]{1,0:T(8,128)}), f32[16384,512]{1,0:T(8,128)}) %all-gather.9.cloned.1.call-update) | async-done | bytes 33554448 | tf_op jit(solution)/shard_map/all_gather | solution.py:17
  258.4 15.1 %reduce_sum.18 = f32[2048,512]{1,0:T(8,128)} reduce(f32[8,2048,512]{2,1,0:T(8,128)} %bitcast.60, f32[]{:T(128)} %constant.147.clone.1), dimensions={0}, to_apply=%region_0.0 | reduce | flops 7340032 | bytes 37748740 | tf_op jit(solution)/shard_map/reduce_sum | solution.py:17
  273.4 11.6 %fusion.42 = f32[512,512]{0,1:T(8,128)} fusion(f32[2048,512]{1,0:T(8,128)} %reduce_sum.18), kind=kOutput, calls=%fused_computation.79 | convolution fusion | flops 6442450944 | bytes 5242880 | tf_op jit(solution)/shard_map/dot_general | solution.py:18
  285.2 51.8 %all-reduce.3.cloned.1.call-done = f32[512,512]{0,1:T(8,128)} async-done(((f32[512,512]{0,1:T(8,128)}), f32[512,512]{0,1:T(8,128)}) %all-reduce.3.cloned.1.call-update) | async-done | bytes 1048592 | tf_op jit(solution)/shard_map/psum | solution.py:19
  340.1 11.7 %cholesky.104 = f32[128,128]{1,0:T(8,128)S(1)} custom-call(f32[128,128]{1,0:T(8,128)S(1)} %cholesky.266), custom_call_target="Cholesky" | custom-call | tf_op jit(solution)/shard_map/jit(cholesky)/cholesky | solution.py:20
  352.0 9.8 %custom-call.31 = f32[1,128,128]{1,2,0:T(8,128)S(1)} custom-call(f32[1,128,128]{2,1,0:T(8,128)S(1)} %get-tuple-element.35), custom_call_target="InvertDiagBlocksLowerTriangular" | custom-call | tf_op jit(solution)/shard_map/jit(cholesky)/cholesky | solution.py:20
  362.4 11.7 %cholesky.217 = f32[128,128]{1,0:T(8,128)S(1)} custom-call(f32[128,128]{1,0:T(8,128)S(1)} %cholesky.270), custom_call_target="Cholesky" | custom-call | tf_op jit(solution)/shard_map/jit(cholesky)/cholesky | solution.py:20
  374.2 10.2 %custom-call.32 = f32[1,128,128]{1,2,0:T(8,128)S(1)} custom-call(f32[1,128,128]{2,1,0:T(8,128)S(1)} %get-tuple-element.32), custom_call_target="InvertDiagBlocksLowerTriangular" | custom-call | tf_op jit(solution)/shard_map/jit(cholesky)/cholesky | solution.py:20
  385.1 11.7 %cholesky.238 = f32[128,128]{1,0:T(8,128)S(1)} custom-call(f32[128,128]{1,0:T(8,128)S(1)} %cholesky.275), custom_call_target="Cholesky" | custom-call | tf_op jit(solution)/shard_map/jit(cholesky)/cholesky | solution.py:20
  397.5 9.8 %custom-call.33 = f32[1,128,128]{1,2,0:T(8,128)S(1)} custom-call(f32[1,128,128]{2,1,0:T(8,128)S(1)} %get-tuple-element.29), custom_call_target="InvertDiagBlocksLowerTriangular" | custom-call | tf_op jit(solution)/shard_map/jit(cholesky)/cholesky | solution.py:20
  407.9 11.7 %cholesky.255 = f32[128,128]{1,0:T(8,128)S(1)} custom-call(f32[128,128]{1,0:T(8,128)S(1)} %convolution_subtract_fusion.4), custom_call_target="Cholesky" | custom-call | tf_op jit(solution)/shard_map/jit(cholesky)/cholesky | solution.py:20
  423.8 10.9 %while.1 = (s32[]{:T(128)}, f32[512,512]{1,0:T(8,128)S(1)}, s32[4,2]{0,1:T(2,128)S(1)}, f32[4,128,128]{2,1,0:T(8,128)}, s32[]{:T(128)}) while((s32[]{:T(128)}, f32[512,512]{1,0:T(8,128)S(1)}, s32[4,2]{0,1:T(2,128)S(1)}, f32[4,128,128]{2,1,0:T(8,128)}, s32[]{:T(128)}) %tuple.33), condition=%wide.while_cond, body=%wide.while_body.sunk | while | flops 2 | bytes 132705 | solution.py:21
  434.8 40.2 %custom-call.34 = f32[4,128,128]{1,2,0:T(8,128)S(1)} custom-call(f32[4,128,128]{2,1,0:T(8,128)} %get-tuple-element.10), custom_call_target="InvertDiagBlocksLowerTriangular" | custom-call | tf_op jit(solution)/shard_map/jit(_solve_triangular)/triangular_solve | solution.py:21
  477.4 3.0 convolution_subtract_fusion.1
  481.6 3.5 convolution_subtract_fusion
  486.2 6.5 fusion.7
  494.8 19.7 %fusion.17 = f32[3328,512]{1,0:T(8,128)} fusion(f32[2048,3328]{1,0:T(8,128)} %param.3, bf16[2048,3328]{1,0:T(8,128)(2,1)} %param.4, f32[128,2048]{1,0:T(8,128)} %fusion.27, f32[128,2048]{1,0:T(8,128)S(1)} %fusion.28, f32[128,2048]{1,0:T(8,128)S(1)} %fusion.30, f32[128,2048]{1,0:T(8,128)S(1)} %fusion.13), kind=kOutput, calls=%fused_computation.30 | convolution fusion | flops 7008157696 | bytes 51904512 | tf_op jit(solution)/shard_map/ic,ir->cr/dot_general | solution.py:24
  514.5 118.7 %reduce-scatter.2.cloned.1.call-done = f32[3328,128]{1,0:T(8,128)} async-done(((f32[3328,512]{1,0:T(8,128)}), f32[3328,128]{1,0:T(8,128)}) %reduce-scatter.2.cloned.1.call-update) | async-done | bytes 1703952 | tf_op jit(solution)/shard_map/reduce_scatter | solution.py:25
  635.1 13.5 %psum.15 = f32[128]{0:T(128)S(1)} all-reduce(f32[128]{0:T(128)S(1)} %multiply_reduce_fusion), channel_id=1, replica_groups=mesh['row'=4,'col'=8] {'col'}, use_global_device_ids=true, to_apply=%region_12.13 | all-reduce | flops 128 | bytes 1024 | tf_op jit(solution)/shard_map/psum | solution.py:26
  648.6 3.7 broadcast_divide_fusion
  656.7 62.1 %all-gather.7.cloned.1.call-done = bf16[3328,512]{1,0:T(8,128)(2,1)} async-done(((bf16[3328,128]{1,0:T(8,128)(2,1)}), bf16[3328,512]{1,0:T(8,128)(2,1)}) %all-gather.7.cloned.1.call-update) | async-done | bytes 3407888 | tf_op jit(solution)/shard_map/all_gather | solution.py:28
  718.8 23.8 %multiply_subtract_fusion = f32[2048,3328]{1,0:T(8,128)} fusion(f32[2048,3328]{1,0:T(8,128)} %param.3, bf16[2048,3328]{1,0:T(8,128)(2,1)} %param.4, bf16[3328,512]{1,0:T(8,128)(2,1)} %all-gather.7.cloned.1.call-done, f32[128,2048]{1,0:T(8,128)} %fusion.27, f32[128,2048]{1,0:T(8,128)S(1)} %fusion.28, f32[128,2048]{1,0:T(8,128)S(1)} %fusion.30, ...), kind=kOutput, calls=%fused_computation.2 | convolution fusion | flops 7014973440 | bytes 75759616 | tf_op jit(solution)/shard_map/ir,cr->ic/dot_general | solution.py:29
  (58 shorter events, 32.5 us)
Async XLA Ops:
  7.2 72.8 %all-gather.5.cloned.1.call-start = ((), (), s32[]{:S(2)}) async-start(), calls=%async_computation.1 | async-start | bytes 4259840 | tf_op jit(solution)/shard_map/all_gather | solution.py:12
  7.9 250.5 %all-gather.9.cloned.1.call-start = ((), (), s32[]{:S(2)}) async-start(), calls=%async_computation.5 | async-start | bytes 37748736 | tf_op jit(solution)/shard_map/all_gather | solution.py:17
  99.4 237.7 %all-reduce.3.cloned.1.call-start = ((), (), s32[]{:S(2)}) async-start(), calls=%async_computation.2 | async-start | bytes 2097152 | tf_op jit(solution)/shard_map/psum | solution.py:19
  285.0 348.2 %reduce-scatter.2.cloned.1.call-start = ((), (), s32[]{:S(2)}) async-start(), calls=%async_computation.3 | async-start | bytes 8519680 | tf_op jit(solution)/shard_map/reduce_scatter | solution.py:25
  434.8 46.8 %copy-start.1 = (f32[512,512]{1,0:T(8,128)}, f32[512,512]{1,0:T(8,128)S(1)}, u32[]{:S(2)}) copy-start(f32[512,512]{1,0:T(8,128)S(1)} %get-tuple-element.101) | copy-start | bytes 3145732
  475.0 6.6 copy-start
  514.5 204.4 %all-gather.7.cloned.1.call-start = ((), (), s32[]{:S(2)}) async-start(), calls=%async_computation.4 | async-start | bytes 4259840 | tf_op jit(solution)/shard_map/all_gather | solution.py:28
Sparse Core Ops, SparseCore 0:
  9.5 70.3 all-gather.4
  99.5 158.8 all-gather.8
  285.1 51.8 all-reduce.2
  514.6 118.5 reduce-scatter.1
  652.4 66.3 all-gather.6
